TPU v7x, 32 devices: a whole 2x2x4 slice. The times are simulated.
32 devices in a mesh: rows: 16 (over z, x, core), chan: 2 (over y).
Axes of the slice: x: 2, y: 2, z: 4, core: 2. Of those that a mesh axis runs over, the one named last changes fastest.
Arguments:
- pixels: float32 [1024, 16384], P(('chan', 'rows')), parts along dimension 0, may hold values from -6 to 6
- row_taps: float32 [32768], P(('chan', 'rows')), parts along dimension 0, may hold values from -0.046875 to 0.046875
- column_taps: float32 [1024], P(('chan', 'rows')), parts along dimension 0, may hold values from -0.25 to 0.25
- stencil: float32 [6, 3], P('chan'), parts along dimension 0, may hold values from -3 to 3
Outputs:
- filtered: float32 [1024, 16384], P(('chan', 'rows')), parts along dimension 0
There are 2 independent parts, one for each index of `chan`. A program takes and returns all parts, laid end to end along the dimension named above; each array names one. Nothing has to cross between parts.
All inputs are finite; a program needn't handle non-finite values.
Results may differ from a plain program's by a relative error of at most 0.0003.
Values sent between devices are 32-bit elements; how exact they have to be, the bound alone decides.
A program may use at most 128 MiB of HBM per device.

v0:
```python
import functools
import math

import jax
import jax.numpy as jnp
import numpy as np
from jax import lax
from jax.experimental import pallas as pl
from jax.experimental.pallas import tpu as pltpu
from jax.sharding import PartitionSpec as P

dft_precision = lax.Precision.HIGH
row_forms = ("kj,rjm->rkm", "rkm,ml->rkl")
column_forms = ("kj,jmc->kmc", "kmc,ml->klc")


def padded_2(cells, sides, width):
    for axis, dim in sides:
        count = lax.axis_size(axis)
        head = lax.slice_in_dim(cells, 0, width, axis=dim)
        tail = lax.slice_in_dim(cells, cells.shape[dim] - width, cells.shape[dim], axis=dim)
        cells = jnp.concatenate(
            [
                lax.ppermute(tail, axis, [(i, (i + 1) % count) for i in range(count)]),
                cells,
                lax.ppermute(head, axis, [((i + 1) % count, i) for i in range(count)]),
            ],
            axis=dim,
        )
    return cells


def split_length(length):
    factor = int(math.isqrt(length))
    while length % factor:
        factor -= 1
    return (length // factor, factor)


def dft_tables(length):
    positions = jnp.arange(length, dtype=jnp.int32)
    product = positions[:, None] * positions[None, :] % length
    angles = product.astype(jnp.float32) * (2.0 * math.pi / length)
    return (jnp.cos(angles), -jnp.sin(angles))


def prepare(length, twist_shape):
    outer_len, inner_len = split_length(length)
    cos_outer, sin_outer = dft_tables(outer_len)
    cos_inner, sin_inner = dft_tables(inner_len)
    outer_pos = jnp.arange(outer_len, dtype=jnp.int32)
    inner_pos = jnp.arange(inner_len, dtype=jnp.int32)
    product = outer_pos[:, None] * inner_pos[None, :] % length
    angles = product.astype(jnp.float32) * (2.0 * math.pi / length)
    twist_real = jnp.cos(angles).reshape(twist_shape)
    twist_imag = (-jnp.sin(angles)).reshape(twist_shape)
    return (
        outer_len,
        inner_len,
        cos_outer,
        sin_outer,
        cos_inner,
        sin_inner,
        twist_real,
        twist_imag,
    )


def contract(form, left, right):
    return jnp.einsum(
        form, left, right, precision=dft_precision, preferred_element_type=jnp.float32
    )


def forward(values, tables, forms):
    outer_len, inner_len, cos_outer, sin_outer, cos_inner, sin_inner, twist_real, twist_imag = (
        tables
    )
    first_real = contract(forms[0], cos_outer, values)
    first_imag = contract(forms[0], sin_outer, values)
    turned_real = first_real * twist_real - first_imag * twist_imag
    turned_imag = first_real * twist_imag + first_imag * twist_real
    out_real = contract(forms[1], turned_real, cos_inner) - contract(
        forms[1], turned_imag, sin_inner
    )
    out_imag = contract(forms[1], turned_real, sin_inner) + contract(
        forms[1], turned_imag, cos_inner
    )
    return (out_real, out_imag)


def inverse(spec_real, spec_imag, tables, forms):
    outer_len, inner_len, cos_outer, sin_outer, cos_inner, sin_inner, twist_real, twist_imag = (
        tables
    )
    back_real = contract(forms[1], spec_real, cos_inner) + contract(forms[1], spec_imag, sin_inner)
    back_imag = contract(forms[1], spec_imag, cos_inner) - contract(forms[1], spec_real, sin_inner)
    turned_real = back_real * twist_real + back_imag * twist_imag
    turned_imag = back_imag * twist_real - back_real * twist_imag
    result = contract(forms[0], cos_outer, turned_real) + contract(forms[0], sin_outer, turned_imag)
    return result / float(outer_len * inner_len)


def convolve(values, filter_spec, tables, forms):
    spec_real, spec_imag = forward(values, tables, forms)
    filter_real, filter_imag = filter_spec
    prod_real = spec_real * filter_real - spec_imag * filter_imag
    prod_imag = spec_real * filter_imag + spec_imag * filter_real
    return inverse(prod_real, prod_imag, tables, forms)


def body(pixels, row_taps, column_taps, stencil):
    rows_dev, row_length = pixels.shape
    devices_rows = lax.axis_size("rows")
    whole_row, whole_column = (
        lax.all_gather(row_taps, "rows", axis=0, tiled=True),
        lax.all_gather(column_taps, "rows", axis=0, tiled=True),
    )
    column_length = whole_column.shape[0]
    row_tables = prepare(row_length, (1, split_length(row_length)[0], split_length(row_length)[1]))
    column_tables = prepare(
        column_length, (split_length(column_length)[0], split_length(column_length)[1], 1)
    )
    row_filter = forward(whole_row.reshape(1, row_tables[0], row_tables[1]), row_tables, row_forms)
    column_filter = forward(
        whole_column.reshape(column_tables[0], column_tables[1], 1), column_tables, column_forms
    )
    cols_dev = row_length // devices_rows
    lane_width = min(128, cols_dev)
    groups = cols_dev // lane_width
    padded = padded_2(pixels, (("rows", 0),), 1)
    shaped = pixels.reshape(pixels.shape[0], row_tables[0], row_tables[1])
    blocks = (
        convolve(shaped, row_filter, row_tables, row_forms)
        .reshape(pixels.shape)
        .reshape(rows_dev, groups, devices_rows * lane_width)
    )
    moved = lax.all_to_all(blocks, "rows", split_axis=2, concat_axis=0, tiled=True)
    shaped = moved.reshape(column_tables[0], column_tables[1], -1)
    result = lax.all_to_all(
        convolve(shaped, column_filter, column_tables, column_forms).reshape(moved.shape),
        "rows",
        split_axis=0,
        concat_axis=2,
        tiled=True,
    )
    convolved = result.reshape(rows_dev, row_length)
    filtered = convolved
    for offset_row in range(3):
        row_band = padded[offset_row : offset_row + rows_dev]
        for offset_col in range(3):
            filtered = filtered + stencil[offset_row, offset_col] * jnp.roll(
                row_band, 1 - offset_col, axis=1
            )
    return filtered


def split_bf16(values):
    high = values.astype(jnp.bfloat16)
    low = (values - high.astype(jnp.float32)).astype(jnp.bfloat16)
    return high, low


def mm(left, right):
    return jnp.dot(left, right, preferred_element_type=jnp.float32)


def mm3(left, right):
    return mm(left[0], right[0]) + (mm(left[0], right[1]) + mm(left[1], right[0]))


def host_tables(side):
    length = side * side
    index = np.arange(side)
    product = index[:, None] * index[None, :]
    angle = 2.0 * np.pi * (product % side) / side
    cos, sin = np.cos(angle), np.sin(angle)
    table = np.block([[cos, sin], [-sin, cos]]).astype(np.float32)

    def halves(array):
        high = array.astype(jnp.bfloat16)
        low = (array - high.astype(np.float32)).astype(jnp.bfloat16)
        return high, low

    fwd_high, fwd_low = halves(table)
    inv_high, inv_low = halves(np.ascontiguousarray(table.T))
    turn = 2.0 * np.pi * product / length
    return (
        fwd_high,
        fwd_low,
        inv_high,
        inv_low,
        np.cos(turn).astype(np.float32),
        (-np.sin(turn)).astype(np.float32),
    )


def kernel(
    dims,
    pixels,
    row_taps,
    column_taps,
    stencil,
    tables_in,
    twists_in,
    out,
    padded,
    tables,
    twists,
    top_row,
    bottom_row,
    recv,
    recv_high,
    recv_low,
    ready,
    back,
    cells_by_row,
    halo_above,
    halo_below,
    all_row,
    all_column,
    circ_high,
    circ_low,
    filter_real,
    filter_imag,
    send_px,
    recv_px,
    send_row,
    recv_row,
    send_col,
    recv_col,
    send_halo,
    recv_halo,
    send_back,
    recv_back,
    send_last,
    recv_last,
    local_sem,
):
    count, rows_dev, side, pieces = dims
    groups = rows_dev // 8
    cols_dev = side * side // count
    a_dev = cols_dev // 128
    column_length = count * rows_dev
    piece_cols = cols_dev // pieces
    own = slice(8, 8 + rows_dev)
    me = lax.axis_index("rows")

    planes = count // 4
    plane, core = me // 4, lax.rem(me, 2)
    way = jnp.where(plane < planes // 2, 1, planes - 1)

    def near(step):
        return plane * 4 + lax.rem(me + step, 4)

    def far(step):
        hop, turn = step % (planes - 1) + 1, step // (planes - 1)
        hop = lax.rem(hop + core * 1 - 1, planes - 1) + 1
        return lax.rem(plane + way * hop, planes) * 4 + lax.rem(me + turn, 4)

    def to_all(start):
        @pl.loop(1, 4)
        def _(step):
            start(near(step))

        @pl.loop(0, count - 4)
        def _(step):
            start(far(step))

    def peer(step):
        return lax.rem(me + step, count)

    load_px = pltpu.make_async_copy(pixels, padded.at[own, :], local_sem.at[0])
    load_tables = pltpu.make_async_copy(tables_in, tables, local_sem.at[1])
    load_twists = pltpu.make_async_copy(twists_in, twists, local_sem.at[2])
    load_px.start()
    load_tables.start()
    load_twists.start()

    barrier = pltpu.get_barrier_semaphore()

    @pl.loop(1, count)
    def _(step):
        pl.semaphore_signal(barrier, inc=1, device_id={"rows": peer(step)})

    pl.semaphore_wait(barrier, count - 1)

    def columns_of(rank, piece):
        return pl.ds(pl.multiple_of(rank * cols_dev + piece * piece_cols, 128), piece_cols)

    def rows_of(rank):
        return pl.ds(pl.multiple_of(rank * rows_dev, 16), rows_dev)

    def px_copy(piece, to, source):
        return pltpu.make_async_remote_copy(
            src_ref=padded.at[own, columns_of(to, piece)],
            dst_ref=recv.at[piece, rows_of(me), :],
            send_sem=send_px.at[piece, to],
            recv_sem=recv_px.at[piece, source],
            device_id={"rows": to},
        )

    def row_copy(to, source):
        return pltpu.make_async_remote_copy(
            src_ref=row_taps,
            dst_ref=all_row.at[me],
            send_sem=send_row.at[to],
            recv_sem=recv_row.at[source],
            device_id={"rows": to},
        )

    def col_copy(to, source):
        return pltpu.make_async_remote_copy(
            src_ref=column_taps,
            dst_ref=all_column.at[me],
            send_sem=send_col.at[to],
            recv_sem=recv_col.at[source],
            device_id={"rows": to},
        )

    def halo_copy(which):
        return pltpu.make_async_remote_copy(
            src_ref=(bottom_row, top_row)[which],
            dst_ref=(halo_above, halo_below)[which],
            send_sem=send_halo.at[which],
            recv_sem=recv_halo.at[which],
            device_id={"rows": peer(1 if which == 0 else count - 1)},
        )

    load_px.wait()

    def first_out(to):
        px_copy(0, to, me).start()
        col_copy(to, me).start()

    to_all(first_out)

    top_row[...] = padded[8:9, :]
    bottom_row[...] = padded[7 + rows_dev : 8 + rows_dev, :]
    halo_copy(0).start()
    halo_copy(1).start()

    to_all(lambda to: row_copy(to, me).start())

    for piece in range(1, pieces):
        to_all(lambda to, piece=piece: px_copy(piece, to, me).start())

    all_row[me] = row_taps[...]
    all_column[me] = column_taps[...]
    load_tables.wait()
    load_twists.wait()

    @pl.loop(1, count)
    def _(step):
        col_copy(peer(step), peer(step)).wait_recv()

    per_block = 128 // rows_dev
    lines = []
    for block in reversed(range(column_length // 128)):
        total = all_column[block * per_block]
        for rank in range(block * per_block + 1, (block + 1) * per_block):
            total = total + all_column[rank]
        lines.append(total)
    line = jnp.concatenate(lines, axis=1)
    line = jnp.broadcast_to(line, (128, column_length))
    turned = [
        pltpu.roll(line, block * 128 + 1, 1, stride=1, stride_axis=0)
        for block in range(column_length // 128)
    ]
    for group in range(groups):
        part = jnp.concatenate(
            [
                turned[rank // per_block][
                    (rank % per_block) * rows_dev + group * 8 :
                    (rank % per_block) * rows_dev + group * 8 + 8
                ]
                for rank in range(count)
            ],
            axis=0,
        )
        high, low = split_bf16(part)
        circ_high[group] = high
        circ_low[group] = low

    forward_table = (0, 1)
    inverse_table = (2, 3)

    def loaded(table):
        return (tables[table[0]], tables[table[1]])

    def swap(real, imag):
        return jnp.concatenate(
            [
                jnp.concatenate([real[:, :side], imag[:, :side]], axis=1),
                jnp.concatenate([real[:, side:], imag[:, side:]], axis=1),
            ],
            axis=0,
        )

    def spectrum(cells):
        first = mm3(loaded(forward_table), split_bf16(cells))
        real, imag = first[:side], first[side:]
        turn_r = jnp.concatenate([twists[0]] * 2, axis=1)
        turn_i = jnp.concatenate([twists[1]] * 2, axis=1)
        turned_cells = swap(real * turn_r - imag * turn_i, real * turn_i + imag * turn_r)
        return mm3(split_bf16(turned_cells), loaded(inverse_table))

    def inverse_of(real, imag):
        cells = jnp.concatenate([real, imag], axis=1)
        first = mm3(split_bf16(cells), loaded(forward_table))
        real, imag = first[:, :side], first[:, side:]
        turn_r = jnp.concatenate([twists[0]] * 2, axis=0)
        turn_i = jnp.concatenate([twists[1]] * 2, axis=0)
        back_real = real * turn_r + imag * turn_i
        back_imag = imag * turn_r - real * turn_i
        cells = jnp.concatenate(
            [
                jnp.concatenate([back_real[:side], back_real[side:]], axis=1),
                jnp.concatenate([back_imag[:side], back_imag[side:]], axis=1),
            ],
            axis=0,
        )
        return mm3(loaded(inverse_table), split_bf16(cells))

    def filter_spectrum():
        @pl.loop(1, count)
        def _(step):
            row_copy(peer(step), peer(step)).wait_recv()

        row_filter = jnp.concatenate([all_row[rank] for rank in range(count)], axis=0)
        nothing = jnp.zeros_like(row_filter)
        filter_spec = spectrum(
            jnp.concatenate(
                [
                    jnp.concatenate([row_filter, nothing], axis=1),
                    jnp.concatenate([nothing, nothing], axis=1),
                ],
                axis=0,
            )
        )[:side]
        filter_real[...] = filter_spec[:, :side] * (1.0 / (side * side))
        filter_imag[...] = filter_spec[:, side:] * (1.0 / (side * side))

    def add_stencil():
        halo_copy(0).wait_recv()
        halo_copy(1).wait_recv()
        padded[7:8, :] = halo_above[...]
        padded[8 + rows_dev : 9 + rows_dev, :] = halo_below[...]
        width = side * side
        for group in range(groups):
            base = group * 8
            above = padded[7 + base : 15 + base, :]
            here = padded[8 + base : 16 + base, :]
            below = padded[9 + base : 17 + base, :]
            sums = [
                stencil[0, b] * above + stencil[1, b] * here + stencil[2, b] * below
                for b in range(3)
            ]
            out[base : base + 8, :] = (
                sums[1] + pltpu.roll(sums[0], 1, 1) + pltpu.roll(sums[2], width - 1, 1)
            )

    def back_copy(piece, to, source):
        return pltpu.make_async_remote_copy(
            src_ref=ready.at[piece, rows_of(to), :],
            dst_ref=back.at[:, columns_of(me, piece)],
            send_sem=send_back.at[piece, to],
            recv_sem=recv_back.at[piece, source],
            device_id={"rows": to},
        )

    last = pieces - 1

    def last_copy(group, to, source):
        return pltpu.make_async_remote_copy(
            src_ref=ready.at[last, pl.ds(pl.multiple_of(to * rows_dev + group * 8, 8), 8), :],
            dst_ref=back.at[pl.ds(group * 8, 8), columns_of(me, last)],
            send_sem=send_last.at[group, to],
            recv_sem=recv_last.at[group, source],
            device_id={"rows": to},
        )

    def take(piece, rank, values):
        at = rows_of(rank)
        high, low = split_bf16(values)
        recv_high[piece, at, :] = high
        recv_low[piece, at, :] = low

    def filtered_rows(piece, group):
        return mm3(
            (circ_high[group], circ_low[group]), (recv_high[piece], recv_low[piece])
        )

    for piece in range(pieces):
        take(piece, me, padded[own, columns_of(me, piece)])

    for piece in range(pieces):

        @pl.loop(1, count)
        def _(step, piece=piece):
            source = peer(step)
            px_copy(piece, source, source).wait_recv()
            take(piece, source, recv[piece, rows_of(source), :])

        for group in range(groups):
            done = filtered_rows(piece, group)
            for rank in range(count):
                at = rank * rows_dev + group * 8
                ready[piece, at : at + 8, :] = done[rank * 8 : rank * 8 + 8]
            if piece == last:
                to_all(lambda to, group=group: last_copy(group, to, me).start())

        if piece != last:
            to_all(lambda to, piece=piece: back_copy(piece, to, me).start())

        back[:, columns_of(me, piece)] = ready[piece, rows_of(me), :]
        if piece == 0:
            filter_spectrum()
            add_stencil()

    flat_cells = cells_by_row.reshape(rows_dev * side, side)
    for piece in range(last):

        @pl.loop(1, count)
        def _(step, piece=piece):
            back_copy(piece, peer(step), peer(step)).wait_recv()

    for group in range(groups):

        @pl.loop(1, count)
        def _(step, group=group):
            last_copy(group, peer(step), peer(step)).wait_recv()

        for a in range(side):
            flat_cells[pl.ds(group * 8 * side + a, 8, stride=side), :] = back[
                group * 8 : group * 8 + 8, a * side : (a + 1) * side
            ]
        for half in range(2):
            row = group * 8 + half * 4
            cells = jnp.concatenate(
                [
                    jnp.concatenate([cells_by_row[row], cells_by_row[row + 2]], axis=1),
                    jnp.concatenate([cells_by_row[row + 1], cells_by_row[row + 3]], axis=1),
                ],
                axis=0,
            )
            spec = spectrum(cells)
            real, imag = spec[:, :side], spec[:, side:]
            filt_r = jnp.concatenate([filter_real[...]] * 2, axis=0)
            filt_i = jnp.concatenate([filter_imag[...]] * 2, axis=0)
            done = inverse_of(real * filt_r - imag * filt_i, real * filt_i + imag * filt_r)
            cells_by_row[row] = done[:side, :side]
            cells_by_row[row + 1] = done[side:, :side]
            cells_by_row[row + 2] = done[:side, side:]
            cells_by_row[row + 3] = done[side:, side:]
        for a in range(side):
            cut = slice(a * side, (a + 1) * side)
            out[group * 8 : group * 8 + 8, cut] += flat_cells[
                pl.ds(group * 8 * side + a, 8, stride=side), :
            ]

    halo_copy(0).wait_send()
    halo_copy(1).wait_send()

    @pl.loop(1, count)
    def _(step):
        row_copy(peer(step), peer(step)).wait_send()
        col_copy(peer(step), peer(step)).wait_send()
        for piece in range(pieces):
            px_copy(piece, peer(step), peer(step)).wait_send()
        for piece in range(last):
            back_copy(piece, peer(step), peer(step)).wait_send()
        for group in range(groups):
            last_copy(group, peer(step), peer(step)).wait_send()


def fits(pixels, row_taps, column_taps):
    rows_dev, row_length = pixels.shape
    count = lax.axis_size("rows")
    side = math.isqrt(row_length)
    return (
        side == 128
        and side * side == row_length
        and row_length % (count * 1024) == 0
        and rows_dev % 16 == 0
        and 128 % rows_dev == 0
        and (count * rows_dev) % 128 == 0
        and count % (128 // rows_dev) == 0
        and count % 4 == 0
        and count > 8
    )


def fused(pixels, row_taps, column_taps, stencil):
    rows_dev, row_length = pixels.shape
    count = lax.axis_size("rows")
    side = math.isqrt(row_length)
    column_length = rows_dev * count
    cols_dev = row_length // count
    a_dev = cols_dev // 128
    groups = rows_dev // 8
    me = lax.axis_index("rows")
    pieces = 2
    piece_cols = cols_dev // pieces
    per_block = 128 // rows_dev
    start = (per_block - 1 - me % per_block) * rows_dev
    wanted = start + rows_dev - 1 - jnp.arange(128, dtype=jnp.int32)
    held = jnp.arange(rows_dev, dtype=jnp.int32)
    placed = jnp.sum(
        jnp.where(wanted[:, None] == held[None, :], column_taps[None, :], 0.0), axis=1
    ).reshape(1, 128)
    made = host_tables(side)
    tables = jnp.asarray(np.stack(made[:4]))
    twists = jnp.asarray(np.stack(made[4:]))
    hbm = pl.BlockSpec(memory_space=pl.ANY)
    vmem = pl.BlockSpec(memory_space=pltpu.VMEM)
    f32, bf16 = jnp.float32, jnp.bfloat16
    dma = pltpu.SemaphoreType.DMA
    return pl.pallas_call(
        functools.partial(kernel, (count, rows_dev, side, pieces)),
        out_shape=jax.ShapeDtypeStruct(pixels.shape, f32),
        in_specs=[hbm, vmem, vmem, pl.BlockSpec(memory_space=pltpu.SMEM), hbm, hbm],
        out_specs=vmem,
        scratch_shapes=[
            pltpu.VMEM((rows_dev + 16, row_length), f32),
            pltpu.VMEM(tables.shape, bf16),
            pltpu.VMEM(twists.shape, f32),
            pltpu.VMEM((1, row_length), f32),
            pltpu.VMEM((1, row_length), f32),
            pltpu.VMEM((pieces, column_length, piece_cols), f32),
            pltpu.VMEM((pieces, column_length, piece_cols), bf16),
            pltpu.VMEM((pieces, column_length, piece_cols), bf16),
            pltpu.VMEM((pieces, column_length, piece_cols), f32),
            pltpu.VMEM((rows_dev, row_length), f32),
            pltpu.VMEM((rows_dev, side, side), f32),
            pltpu.VMEM((1, row_length), f32),
            pltpu.VMEM((1, row_length), f32),
            pltpu.VMEM((count, a_dev, 128), f32),
            pltpu.VMEM((count, 1, 128), f32),
            pltpu.VMEM((groups, count * 8, column_length), bf16),
            pltpu.VMEM((groups, count * 8, column_length), bf16),
            pltpu.VMEM((side, side), f32),
            pltpu.VMEM((side, side), f32),
            dma((pieces, count)),
            dma((pieces, count)),
            dma((count,)),
            dma((count,)),
            dma((count,)),
            dma((count,)),
            dma((2,)),
            dma((2,)),
            dma((pieces, count)),
            dma((pieces, count)),
            dma((groups, count)),
            dma((groups, count)),
            dma((3,)),
        ],
        compiler_params=pltpu.CompilerParams(
            collective_id=0, has_side_effects=True, vmem_limit_bytes=60 * 1024 * 1024
        ),
    )(pixels, row_taps.reshape(a_dev, 128), placed, stencil, tables, twists)


def chosen(pixels, row_taps, column_taps, stencil):
    if fits(pixels, row_taps, column_taps):
        return fused(pixels, row_taps, column_taps, stencil)
    return body(pixels, row_taps, column_taps, stencil)


def solution(mesh):
    in_specs = (
        P(("chan", "rows"), None),
        P(("chan", "rows")),
        P(("chan", "rows")),
        P("chan", None),
    )
    out_specs = P(("chan", "rows"), None)
    return jax.shard_map(chosen, mesh=mesh, in_specs=in_specs, out_specs=out_specs, check_vma=False)
```

profile of v0, /device:TPU:0, one launch (start us, length us, event | category | flops | bytes accessed | tf_op | source)
XLA Modules:
  0.0 112.3 jit_solution(5031145912430732451)
XLA Ops:
  0.0 1.3 %select_reduce_fusion = f32[128]{0:T(128)} fusion(f32[32]{0:T(128)} %param.8, s32[128]{0:T(128)S(1)} %iota_subtract_fusion), kind=kLoop, calls=%fused_computation | loop fusion | flops 12160 | bytes 1152 | tf_op jit(solution)/shard_map/reduce_sum | solution.py:609
  1.3 107.9 %shard_map.64 = f32[32,16384]{1,0:T(8,128)} custom-call(f32[32,16384]{1,0:T(8,128)} %pixels.1, f32[8,128]{1,0:T(8,128)} %bitcast.2, f32[1,128]{1,0:T(1,128)} %bitcast.3, f32[3,3]{1,0:T(4,128)} %stencil.1, bf16[4,256,256]{2,1,0:T(8,128)(2,1)} %constant.32.clone.tables_in, f32[2,128,128]{2,1,0:T(8,128)} %constant.33.clone.twists_in), custom_call_target="tpu_custom_call" | custom-call | tf_op jit(solution)/shard_map/pallas_call | solution.py:619
  109.2 3.0 %copy.8 = f32[32,16384]{1,0:T(8,128)} copy(f32[32,16384]{1,0:T(8,128)} %shard_map.64) | data formatting | bytes 4194304
  (1 shorter events, 0.0 us)
where the time goes:
time: 113 us; the launch traced here: 112 us
  Pallas kernels  108 us (96%)
  local copies, waits for them, and re-layouts  3.05 us (3%)
  other arithmetic  1.25 us (1%)
    pallas_call x1, Pallas kernels, fused(): pl.pallas_call(functools.partial(kernel, (count, rows_dev, side, pieces))...  108 us
    unnamed x1, local copies, waits for them, and re-layouts  3.05 us

commit v1 on v0

--- a/solution.py
+++ b/solution.py
@@ -200,7 +200,7 @@
     pixels,
     row_taps,
     column_taps,
-    stencil,
+    stencil_in,
     tables_in,
     twists_in,
     out,
@@ -210,8 +210,8 @@
     top_row,
     bottom_row,
     recv,
-    recv_high,
-    recv_low,
+    part_high,
+    part_low,
     ready,
     back,
     cells_by_row,
@@ -223,18 +223,16 @@
     circ_low,
     filter_real,
     filter_imag,
+    stencil,
     send_px,
     recv_px,
-    send_row,
+    send_taps,
     recv_row,
-    send_col,
     recv_col,
     send_halo,
     recv_halo,
     send_back,
     recv_back,
-    send_last,
-    recv_last,
     local_sem,
 ):
     count, rows_dev, side, pieces = dims
@@ -243,39 +241,51 @@
     a_dev = cols_dev // 128
     column_length = count * rows_dev
     piece_cols = cols_dev // pieces
+    last = pieces - 1
     own = slice(8, 8 + rows_dev)
     me = lax.axis_index("rows")
-
-    planes = count // 4
-    plane, core = me // 4, lax.rem(me, 2)
-    way = jnp.where(plane < planes // 2, 1, planes - 1)
-
-    def near(step):
-        return plane * 4 + lax.rem(me + step, 4)
-
-    def far(step):
-        hop, turn = step % (planes - 1) + 1, step // (planes - 1)
-        hop = lax.rem(hop + core * 1 - 1, planes - 1) + 1
-        return lax.rem(plane + way * hop, planes) * 4 + lax.rem(me + turn, 4)
-
-    def to_all(start):
-        @pl.loop(1, 4)
-        def _(step):
-            start(near(step))
-
-        @pl.loop(0, count - 4)
-        def _(step):
-            start(far(step))
+    plane, spot = me // 4, lax.rem(me, 4)
+    x, core = spot // 2, lax.rem(me, 2)
+    low_half = plane < 2
+    outer = (plane == 0) | (plane == 3)
+    inner = jnp.logical_not(outer)
+    first = jnp.where(low_half, core, 1 - core)
+
+    def cross(step):
+        turn = lax.rem(step // 4 + first, 2)
+        depth = lax.rem(step // 2, 2)
+        plane_to = jnp.where(low_half, 3 - depth, depth)
+        return plane_to * 4 + lax.rem(x + turn, 2) * 2 + lax.rem(core + step, 2)
+
+    def beside(step):
+        plane_to = plane + 1 - 2 * lax.rem(plane, 2)
+        return plane_to * 4 + lax.rem(x + step // 2, 2) * 2 + lax.rem(core + step, 2)
+
+    def level(step):
+        return plane * 4 + lax.rem(spot + 1 + step, 4)
 
     def peer(step):
         return lax.rem(me + step, count)
 
-    load_px = pltpu.make_async_copy(pixels, padded.at[own, :], local_sem.at[0])
-    load_tables = pltpu.make_async_copy(tables_in, tables, local_sem.at[1])
-    load_twists = pltpu.make_async_copy(twists_in, twists, local_sem.at[2])
-    load_px.start()
-    load_tables.start()
-    load_twists.start()
+    def over_cross(start):
+        @pl.loop(0, 8)
+        def _(step):
+            start(cross(step))
+
+    def over_beside(start):
+        @pl.loop(0, 4)
+        def _(step):
+            start(beside(step))
+
+    def over_level(start):
+        @pl.loop(0, 3)
+        def _(step):
+            start(level(step))
+
+    def over_all(start):
+        over_cross(start)
+        over_beside(start)
+        over_level(start)
 
     barrier = pltpu.get_barrier_semaphore()
 
@@ -283,37 +293,61 @@
     def _(step):
         pl.semaphore_signal(barrier, inc=1, device_id={"rows": peer(step)})
 
-    pl.semaphore_wait(barrier, count - 1)
+    load_px = pltpu.make_async_copy(pixels, padded.at[own, :], local_sem.at[0])
+    load_col = pltpu.make_async_copy(column_taps, all_column.at[me], local_sem.at[3])
+    load_row = pltpu.make_async_copy(row_taps, all_row.at[me], local_sem.at[4])
+    load_tables = pltpu.make_async_copy(tables_in, tables, local_sem.at[1])
+    load_twists = pltpu.make_async_copy(twists_in, twists, local_sem.at[2])
+    load_stencil = pltpu.make_async_copy(stencil_in, stencil, local_sem.at[5])
+    load_col.start()
+    load_px.start()
+    load_row.start()
+    load_tables.start()
+    load_twists.start()
+    load_stencil.start()
 
     def columns_of(rank, piece):
         return pl.ds(pl.multiple_of(rank * cols_dev + piece * piece_cols, 128), piece_cols)
 
+    def all_columns_of(rank):
+        return pl.ds(pl.multiple_of(rank * cols_dev, 128), cols_dev)
+
     def rows_of(rank):
         return pl.ds(pl.multiple_of(rank * rows_dev, 16), rows_dev)
 
-    def px_copy(piece, to, source):
-        return pltpu.make_async_remote_copy(
+    def px_start(piece, to):
+        pltpu.make_async_remote_copy(
             src_ref=padded.at[own, columns_of(to, piece)],
             dst_ref=recv.at[piece, rows_of(me), :],
-            send_sem=send_px.at[piece, to],
-            recv_sem=recv_px.at[piece, source],
+            send_sem=send_px,
+            recv_sem=recv_px.at[piece],
             device_id={"rows": to},
+        ).start()
+
+    def px_all(piece):
+        held = recv.at[piece, pl.ds(0, column_length - rows_dev), :]
+        return pltpu.make_async_remote_copy(
+            src_ref=held,
+            dst_ref=held,
+            send_sem=send_px,
+            recv_sem=recv_px.at[piece],
+            device_id={"rows": peer(1)},
         )
 
     def row_copy(to, source):
         return pltpu.make_async_remote_copy(
-            src_ref=row_taps,
+            src_ref=all_row.at[me],
             dst_ref=all_row.at[me],
-            send_sem=send_row.at[to],
+            send_sem=send_taps.at[0, to],
             recv_sem=recv_row.at[source],
             device_id={"rows": to},
         )
 
     def col_copy(to, source):
         return pltpu.make_async_remote_copy(
-            src_ref=column_taps,
+            src_ref=all_column.at[me],
             dst_ref=all_column.at[me],
-            send_sem=send_col.at[to],
+            send_sem=send_taps.at[1, to],
             recv_sem=recv_col.at[source],
             device_id={"rows": to},
         )
@@ -327,60 +361,90 @@
             device_id={"rows": peer(1 if which == 0 else count - 1)},
         )
 
-    load_px.wait()
-
-    def first_out(to):
-        px_copy(0, to, me).start()
-        col_copy(to, me).start()
-
-    to_all(first_out)
+    def cross_px(piece):
+        if piece < pieces:
+            over_cross(lambda to: px_start(piece, to))
+
+    def beside_px(piece):
+        if piece < pieces:
+            over_beside(lambda to: px_start(piece, to))
+
+    def level_px(piece):
+        over_level(lambda to: px_start(piece, to))
+
+    with jax.named_scope("barrier"):
+        pl.semaphore_wait(barrier, count - 1)
+    with jax.named_scope("loadpx"):
+        load_col.wait()
+        load_px.wait()
+
+    over_all(lambda to: col_copy(to, me).start())
+    cross_px(0)
+    beside_px(0)
+    level_px(0)
 
     top_row[...] = padded[8:9, :]
     bottom_row[...] = padded[7 + rows_dev : 8 + rows_dev, :]
     halo_copy(0).start()
     halo_copy(1).start()
-
-    to_all(lambda to: row_copy(to, me).start())
+    load_row.wait()
+    over_all(lambda to: row_copy(to, me).start())
+
+    @pl.when(outer)
+    def _():
+        beside_px(1)
+
+    @pl.when(inner)
+    def _():
+        for piece in range(1, pieces):
+            cross_px(piece)
+            beside_px(piece)
 
     for piece in range(1, pieces):
-        to_all(lambda to, piece=piece: px_copy(piece, to, me).start())
-
-    all_row[me] = row_taps[...]
-    all_column[me] = column_taps[...]
+        level_px(piece)
+
+    for piece in range(pieces):
+        recv[piece, rows_of(me), :] = padded[own, columns_of(me, piece)]
     load_tables.wait()
     load_twists.wait()
-
-    @pl.loop(1, count)
-    def _(step):
-        col_copy(peer(step), peer(step)).wait_recv()
+    load_stencil.wait()
+
+    with jax.named_scope("waitcol"):
+
+        @pl.loop(1, count)
+        def _(step):
+            col_copy(peer(step), peer(step)).wait_recv()
 
     per_block = 128 // rows_dev
+    taps = jnp.concatenate([all_column[rank] for rank in range(count)], axis=0)
+    held_at = lax.broadcasted_iota(jnp.int32, (rows_dev, 128), 0)
+    lane = lax.broadcasted_iota(jnp.int32, (rows_dev, 128), 1)
+    placed = []
+    for spot_in in range(per_block):
+        start = (per_block - 1 - spot_in) * rows_dev
+        chosen_lane = jnp.where(lane == start + rows_dev - 1 - held_at, 1.0, 0.0)
+        placed.append(
+            jnp.dot(
+                taps,
+                chosen_lane,
+                precision=lax.Precision.HIGHEST,
+                preferred_element_type=jnp.float32,
+            )
+        )
     lines = []
     for block in reversed(range(column_length // 128)):
-        total = all_column[block * per_block]
-        for rank in range(block * per_block + 1, (block + 1) * per_block):
-            total = total + all_column[rank]
+        total = placed[0][block * per_block : block * per_block + 1]
+        for spot_in in range(1, per_block):
+            rank = block * per_block + spot_in
+            total = total + placed[spot_in][rank : rank + 1]
         lines.append(total)
     line = jnp.concatenate(lines, axis=1)
     line = jnp.broadcast_to(line, (128, column_length))
-    turned = [
-        pltpu.roll(line, block * 128 + 1, 1, stride=1, stride_axis=0)
-        for block in range(column_length // 128)
-    ]
-    for group in range(groups):
-        part = jnp.concatenate(
-            [
-                turned[rank // per_block][
-                    (rank % per_block) * rows_dev + group * 8 :
-                    (rank % per_block) * rows_dev + group * 8 + 8
-                ]
-                for rank in range(count)
-            ],
-            axis=0,
-        )
-        high, low = split_bf16(part)
-        circ_high[group] = high
-        circ_low[group] = low
+    for block in range(column_length // 128):
+        turned = pltpu.roll(line, block * 128 + 1, 1, stride=1, stride_axis=0)
+        high, low = split_bf16(turned)
+        circ_high[block * 128 : block * 128 + 128, :] = high
+        circ_low[block * 128 : block * 128 + 128, :] = low
 
     forward_table = (0, 1)
     inverse_table = (2, 3)
@@ -460,118 +524,142 @@
                 sums[1] + pltpu.roll(sums[0], 1, 1) + pltpu.roll(sums[2], width - 1, 1)
             )
 
-    def back_copy(piece, to, source):
+    def back_start(group, to, pieces_from, pieces_to):
+        width = (pieces_to - pieces_from) * piece_cols
+        at = pieces_from * piece_cols
+        pltpu.make_async_remote_copy(
+            src_ref=ready.at[
+                pl.ds(pl.multiple_of(to * rows_dev + group * 8, 8), 8), pl.ds(at, width)
+            ],
+            dst_ref=back.at[
+                pl.ds(group * 8, 8), pl.ds(pl.multiple_of(me * cols_dev + at, 128), width)
+            ],
+            send_sem=send_back,
+            recv_sem=recv_back.at[group],
+            device_id={"rows": to},
+        ).start()
+
+    def back_all(group):
+        held = back.at[pl.ds(group * 8, 8), pl.ds(0, (count - 1) * cols_dev)]
         return pltpu.make_async_remote_copy(
-            src_ref=ready.at[piece, rows_of(to), :],
-            dst_ref=back.at[:, columns_of(me, piece)],
-            send_sem=send_back.at[piece, to],
-            recv_sem=recv_back.at[piece, source],
-            device_id={"rows": to},
-        )
-
-    last = pieces - 1
-
-    def last_copy(group, to, source):
-        return pltpu.make_async_remote_copy(
-            src_ref=ready.at[last, pl.ds(pl.multiple_of(to * rows_dev + group * 8, 8), 8), :],
-            dst_ref=back.at[pl.ds(group * 8, 8), columns_of(me, last)],
-            send_sem=send_last.at[group, to],
-            recv_sem=recv_last.at[group, source],
-            device_id={"rows": to},
-        )
-
-    def take(piece, rank, values):
-        at = rows_of(rank)
-        high, low = split_bf16(values)
-        recv_high[piece, at, :] = high
-        recv_low[piece, at, :] = low
-
-    def filtered_rows(piece, group):
-        return mm3(
-            (circ_high[group], circ_low[group]), (recv_high[piece], recv_low[piece])
-        )
+            src_ref=held,
+            dst_ref=held,
+            send_sem=send_back,
+            recv_sem=recv_back.at[group],
+            device_id={"rows": peer(1)},
+        )
+
+    def rest(group):
+        def start(to):
+            back_start(group, to, last if group == 0 else 0, pieces)
+
+        return start
+
+    def early(piece):
+        over_all(lambda to: back_start(0, to, piece, piece + 1))
 
     for piece in range(pieces):
-        take(piece, me, padded[own, columns_of(me, piece)])
-
-    for piece in range(pieces):
+        with jax.named_scope(f"waitpx#p={piece}"):
+            px_all(piece).wait_recv()
+
+        @pl.when(outer)
+        def _(piece=piece):
+            cross_px(piece + 1)
+            beside_px(piece + 2)
+            if piece == last:
+                for sent in range(last):
+                    early(sent)
+
+        with jax.named_scope(f"mm#p={piece}"):
+            high, low = split_bf16(recv[piece])
+            part_high[...] = high
+            part_low[...] = low
+            at = slice(piece * piece_cols, (piece + 1) * piece_cols)
+            ready[:, at] = mm3(
+                (circ_high[...], circ_low[...]), (part_high[...], part_low[...])
+            )
+        if piece != last:
+
+            @pl.when(inner)
+            def _(piece=piece):
+                early(piece)
+
+        if piece == 0:
+            with jax.named_scope("stencil"):
+                add_stencil()
+        if piece == 1:
+            with jax.named_scope("filtspec"):
+                filter_spectrum()
+
+    @pl.when(outer)
+    def _():
+        over_cross(rest(0))
+        over_beside(rest(0))
+        over_beside(rest(1))
+
+    @pl.when(inner)
+    def _():
+        for group in range(groups):
+            over_cross(rest(group))
+            over_beside(rest(group))
+
+    for group in range(groups):
+        over_level(rest(group))
+    back[:, all_columns_of(me)] = ready[rows_of(me), :]
+
+    flat_cells = cells_by_row.reshape(rows_dev * side, side)
+    for group in range(groups):
+        with jax.named_scope(f"waitback#g={group}"):
+            back_all(group).wait_recv()
+
+        @pl.when(outer)
+        def _(group=group):
+            if group + 1 < groups:
+                over_cross(rest(group + 1))
+            if group + 2 < groups:
+                over_beside(rest(group + 2))
+
+        with jax.named_scope(f"fft#g={group}"):
+            for a in range(side):
+                flat_cells[pl.ds(group * 8 * side + a, 8, stride=side), :] = back[
+                    group * 8 : group * 8 + 8, a * side : (a + 1) * side
+                ]
+            for half in range(2):
+                row = group * 8 + half * 4
+                cells = jnp.concatenate(
+                    [
+                        jnp.concatenate([cells_by_row[row], cells_by_row[row + 2]], axis=1),
+                        jnp.concatenate([cells_by_row[row + 1], cells_by_row[row + 3]], axis=1),
+                    ],
+                    axis=0,
+                )
+                spec = spectrum(cells)
+                real, imag = spec[:, :side], spec[:, side:]
+                filt_r = jnp.concatenate([filter_real[...]] * 2, axis=0)
+                filt_i = jnp.concatenate([filter_imag[...]] * 2, axis=0)
+                done = inverse_of(real * filt_r - imag * filt_i, real * filt_i + imag * filt_r)
+                cells_by_row[row] = done[:side, :side]
+                cells_by_row[row + 1] = done[side:, :side]
+                cells_by_row[row + 2] = done[:side, side:]
+                cells_by_row[row + 3] = done[side:, side:]
+            for a in range(side):
+                cut = slice(a * side, (a + 1) * side)
+                out[group * 8 : group * 8 + 8, cut] += flat_cells[
+                    pl.ds(group * 8 * side + a, 8, stride=side), :
+                ]
+
+    with jax.named_scope("drain"):
+        halo_copy(0).wait_send()
+        halo_copy(1).wait_send()
+        for piece in range(pieces):
+            px_all(piece).wait_send()
+        for group in range(groups):
+            back_all(group).wait_send()
 
         @pl.loop(1, count)
-        def _(step, piece=piece):
-            source = peer(step)
-            px_copy(piece, source, source).wait_recv()
-            take(piece, source, recv[piece, rows_of(source), :])
-
-        for group in range(groups):
-            done = filtered_rows(piece, group)
-            for rank in range(count):
-                at = rank * rows_dev + group * 8
-                ready[piece, at : at + 8, :] = done[rank * 8 : rank * 8 + 8]
-            if piece == last:
-                to_all(lambda to, group=group: last_copy(group, to, me).start())
-
-        if piece != last:
-            to_all(lambda to, piece=piece: back_copy(piece, to, me).start())
-
-        back[:, columns_of(me, piece)] = ready[piece, rows_of(me), :]
-        if piece == 0:
-            filter_spectrum()
-            add_stencil()
-
-    flat_cells = cells_by_row.reshape(rows_dev * side, side)
-    for piece in range(last):
-
-        @pl.loop(1, count)
-        def _(step, piece=piece):
-            back_copy(piece, peer(step), peer(step)).wait_recv()
-
-    for group in range(groups):
-
-        @pl.loop(1, count)
-        def _(step, group=group):
-            last_copy(group, peer(step), peer(step)).wait_recv()
-
-        for a in range(side):
-            flat_cells[pl.ds(group * 8 * side + a, 8, stride=side), :] = back[
-                group * 8 : group * 8 + 8, a * side : (a + 1) * side
-            ]
-        for half in range(2):
-            row = group * 8 + half * 4
-            cells = jnp.concatenate(
-                [
-                    jnp.concatenate([cells_by_row[row], cells_by_row[row + 2]], axis=1),
-                    jnp.concatenate([cells_by_row[row + 1], cells_by_row[row + 3]], axis=1),
-                ],
-                axis=0,
-            )
-            spec = spectrum(cells)
-            real, imag = spec[:, :side], spec[:, side:]
-            filt_r = jnp.concatenate([filter_real[...]] * 2, axis=0)
-            filt_i = jnp.concatenate([filter_imag[...]] * 2, axis=0)
-            done = inverse_of(real * filt_r - imag * filt_i, real * filt_i + imag * filt_r)
-            cells_by_row[row] = done[:side, :side]
-            cells_by_row[row + 1] = done[side:, :side]
-            cells_by_row[row + 2] = done[:side, side:]
-            cells_by_row[row + 3] = done[side:, side:]
-        for a in range(side):
-            cut = slice(a * side, (a + 1) * side)
-            out[group * 8 : group * 8 + 8, cut] += flat_cells[
-                pl.ds(group * 8 * side + a, 8, stride=side), :
-            ]
-
-    halo_copy(0).wait_send()
-    halo_copy(1).wait_send()
-
-    @pl.loop(1, count)
-    def _(step):
-        row_copy(peer(step), peer(step)).wait_send()
-        col_copy(peer(step), peer(step)).wait_send()
-        for piece in range(pieces):
-            px_copy(piece, peer(step), peer(step)).wait_send()
-        for piece in range(last):
-            back_copy(piece, peer(step), peer(step)).wait_send()
-        for group in range(groups):
-            last_copy(group, peer(step), peer(step)).wait_send()
+        def _(step):
+            row_copy(peer(step), peer(step)).wait_send()
+            col_copy(peer(step), peer(step)).wait_send()
 
 
 def fits(pixels, row_taps, column_taps):
@@ -586,8 +674,7 @@
         and 128 % rows_dev == 0
         and (count * rows_dev) % 128 == 0
         and count % (128 // rows_dev) == 0
-        and count % 4 == 0
-        and count > 8
+        and count == 16
     )
 
 
@@ -599,27 +686,19 @@
     cols_dev = row_length // count
     a_dev = cols_dev // 128
     groups = rows_dev // 8
-    me = lax.axis_index("rows")
-    pieces = 2
+    pieces = 4
     piece_cols = cols_dev // pieces
-    per_block = 128 // rows_dev
-    start = (per_block - 1 - me % per_block) * rows_dev
-    wanted = start + rows_dev - 1 - jnp.arange(128, dtype=jnp.int32)
-    held = jnp.arange(rows_dev, dtype=jnp.int32)
-    placed = jnp.sum(
-        jnp.where(wanted[:, None] == held[None, :], column_taps[None, :], 0.0), axis=1
-    ).reshape(1, 128)
     made = host_tables(side)
     tables = jnp.asarray(np.stack(made[:4]))
     twists = jnp.asarray(np.stack(made[4:]))
-    hbm = pl.BlockSpec(memory_space=pl.ANY)
+    hbm = pl.BlockSpec(memory_space=pltpu.HBM)
     vmem = pl.BlockSpec(memory_space=pltpu.VMEM)
     f32, bf16 = jnp.float32, jnp.bfloat16
     dma = pltpu.SemaphoreType.DMA
     return pl.pallas_call(
         functools.partial(kernel, (count, rows_dev, side, pieces)),
         out_shape=jax.ShapeDtypeStruct(pixels.shape, f32),
-        in_specs=[hbm, vmem, vmem, pl.BlockSpec(memory_space=pltpu.SMEM), hbm, hbm],
+        in_specs=[hbm] * 6,
         out_specs=vmem,
         scratch_shapes=[
             pltpu.VMEM((rows_dev + 16, row_length), f32),
@@ -628,37 +707,47 @@
             pltpu.VMEM((1, row_length), f32),
             pltpu.VMEM((1, row_length), f32),
             pltpu.VMEM((pieces, column_length, piece_cols), f32),
-            pltpu.VMEM((pieces, column_length, piece_cols), bf16),
-            pltpu.VMEM((pieces, column_length, piece_cols), bf16),
-            pltpu.VMEM((pieces, column_length, piece_cols), f32),
+            pltpu.VMEM((column_length, piece_cols), bf16),
+            pltpu.VMEM((column_length, piece_cols), bf16),
+            pltpu.VMEM((column_length, cols_dev), f32),
             pltpu.VMEM((rows_dev, row_length), f32),
             pltpu.VMEM((rows_dev, side, side), f32),
             pltpu.VMEM((1, row_length), f32),
             pltpu.VMEM((1, row_length), f32),
             pltpu.VMEM((count, a_dev, 128), f32),
-            pltpu.VMEM((count, 1, 128), f32),
-            pltpu.VMEM((groups, count * 8, column_length), bf16),
-            pltpu.VMEM((groups, count * 8, column_length), bf16),
+            pltpu.VMEM((count, 1, rows_dev), f32),
+            pltpu.VMEM((column_length, column_length), bf16),
+            pltpu.VMEM((column_length, column_length), bf16),
             pltpu.VMEM((side, side), f32),
             pltpu.VMEM((side, side), f32),
-            dma((pieces, count)),
-            dma((pieces, count)),
-            dma((count,)),
-            dma((count,)),
+            pltpu.SMEM((3, 3), f32),
+            dma,
+            dma((pieces,)),
+            dma((2, count)),
             dma((count,)),
             dma((count,)),
             dma((2,)),
             dma((2,)),
-            dma((pieces, count)),
-            dma((pieces, count)),
-            dma((groups, count)),
-            dma((groups, count)),
-            dma((3,)),
+            dma,
+            dma((groups,)),
+            dma((6,)),
         ],
         compiler_params=pltpu.CompilerParams(
-            collective_id=0, has_side_effects=True, vmem_limit_bytes=60 * 1024 * 1024
+            collective_id=0, has_side_effects=True, vmem_limit_bytes=32 * 1024 * 1024
         ),
-    )(pixels, row_taps.reshape(a_dev, 128), placed, stencil, tables, twists)
+    )(
+        *(
+            pltpu.with_memory_space_constraint(operand, pltpu.HBM)
+            for operand in (
+                pixels,
+                row_taps.reshape(a_dev, 128),
+                column_taps.reshape(1, rows_dev),
+                stencil,
+                tables,
+                twists,
+            )
+        )
+    )
 
 
 def chosen(pixels, row_taps, column_taps, stencil):

time: 113 us -> 104 us (0.920)
  Pallas kernels: 108 us -> 102 us
  local copies, waits for them, and re-layouts: 3.05 us -> 1.32 us
  other arithmetic: 1.25 us -> 0 us
    pallas_call x1, Pallas kernels: 108 us -> 102 us  [fused(): pl.pallas_call(functools.partial(kernel, (count, rows_dev, side, pieces))...]
    unnamed x1, local copies, waits for them, and re-layouts: 3.05 us -> 1.32 us
    reduce_sum x1 -> x0, other arithmetic: 1.25 us -> none  [fused(): jnp.sum(jnp.where(wanted[:, None] == held[None, :], column_taps[None, :],...]
where the time goes in v1:
time: 104 us; the launch traced here: 103 us
  Pallas kernels  102 us (98%)
  local copies, waits for them, and re-layouts  1.32 us (1%)
    pallas_call x1, Pallas kernels, fused(): pl.pallas_call(functools.partial(kernel, (count, rows_dev, side, pieces))...  102 us

profile of v1, /device:TPU:0, one launch (start us, length us, event | category | flops | bytes accessed | tf_op | source)
XLA Modules:
  0.0 103.5 jit_solution(5267796889783283038)
XLA Ops:
  0.0 102.1 %shard_map.64 = f32[32,16384]{1,0:T(8,128)S(1)} custom-call(f32[32,16384]{1,0:T(8,128)} %pixels.1, f32[8,128]{1,0:T(8,128)} %bitcast.2, f32[1,32]{1,0:T(1,128)} %bitcast.3, f32[3,3]{1,0:T(4,128)} %stencil_in.1, bf16[4,256,256]{2,1,0:T(8,128)(2,1)} %constant.4.clone.tables_in, f32[2,128,128]{2,1,0:T(8,128)} %constant.5.clone.twists_in), custom_call_target="tpu_custom_call" | custom-call | tf_op jit(solution)/shard_map/pallas_call | solution.py:698
  102.1 1.3 %copy.8 = f32[32,16384]{1,0:T(8,128)} copy(f32[32,16384]{1,0:T(8,128)S(1)} %shard_map.64) | data formatting | bytes 4194304

commit v2 on v1

--- a/solution.py
+++ b/solution.py
@@ -193,6 +193,11 @@
         np.cos(turn).astype(np.float32),
         (-np.sin(turn)).astype(np.float32),
     )
+
+
+def bands_of(rows_dev):
+    whole = [(at, 8) for at in range(0, rows_dev - 8, 8)]
+    return whole + [(rows_dev - 8, 4), (rows_dev - 4, 4)]
 
 
 def kernel(
@@ -226,7 +231,8 @@
     stencil,
     send_px,
     recv_px,
-    send_taps,
+    send_row,
+    send_col,
     recv_row,
     recv_col,
     send_halo,
@@ -234,9 +240,11 @@
     send_back,
     recv_back,
     local_sem,
+    hello,
 ):
     count, rows_dev, side, pieces = dims
-    groups = rows_dev // 8
+    bands = bands_of(rows_dev)
+    groups = len(bands)
     cols_dev = side * side // count
     a_dev = cols_dev // 128
     column_length = count * rows_dev
@@ -252,8 +260,8 @@
     first = jnp.where(low_half, core, 1 - core)
 
     def cross(step):
-        turn = lax.rem(step // 4 + first, 2)
-        depth = lax.rem(step // 2, 2)
+        turn = lax.rem(step // 2 + first, 2)
+        depth = step // 4
         plane_to = jnp.where(low_half, 3 - depth, depth)
         return plane_to * 4 + lax.rem(x + turn, 2) * 2 + lax.rem(core + step, 2)
 
@@ -282,26 +290,49 @@
         def _(step):
             start(level(step))
 
+    def over_half(start):
+        over_beside(start)
+        over_level(start)
+
     def over_all(start):
         over_cross(start)
         over_beside(start)
         over_level(start)
 
+    mirror = lax.rem(me + count // 2, count)
     barrier = pltpu.get_barrier_semaphore()
 
-    @pl.loop(1, count)
-    def _(step):
-        pl.semaphore_signal(barrier, inc=1, device_id={"rows": peer(step)})
-
-    load_px = pltpu.make_async_copy(pixels, padded.at[own, :], local_sem.at[0])
+    over_level(lambda to: pl.semaphore_signal(barrier, inc=1, device_id={"rows": to}))
+
+    @pl.loop((plane + 1) * 4, count)
+    def _(to):
+        pl.semaphore_signal(barrier, inc=1, device_id={"rows": to})
+
+    def load_part(rank, at, width, sem):
+        cut = pl.ds(pl.multiple_of(rank * cols_dev + at, 128), width)
+        return pltpu.make_async_copy(pixels.at[:, cut], padded.at[own, cut], local_sem.at[sem])
+
+    def loaded_px(width, sem):
+        cut = pl.ds(0, count * width)
+        pltpu.make_async_copy(pixels.at[:, cut], padded.at[own, cut], local_sem.at[sem]).wait()
+
     load_col = pltpu.make_async_copy(column_taps, all_column.at[me], local_sem.at[3])
     load_row = pltpu.make_async_copy(row_taps, all_row.at[me], local_sem.at[4])
     load_tables = pltpu.make_async_copy(tables_in, tables, local_sem.at[1])
     load_twists = pltpu.make_async_copy(twists_in, twists, local_sem.at[2])
     load_stencil = pltpu.make_async_copy(stencil_in, stencil, local_sem.at[5])
     load_col.start()
-    load_px.start()
+
+    @pl.loop(0, count)
+    def _(rank):
+        load_part(rank, 0, piece_cols, 0).start()
+
     load_row.start()
+
+    @pl.loop(0, count)
+    def _(rank):
+        load_part(rank, piece_cols, cols_dev - piece_cols, 6).start()
+
     load_tables.start()
     load_twists.start()
     load_stencil.start()
@@ -334,22 +365,51 @@
             device_id={"rows": peer(1)},
         )
 
-    def row_copy(to, source):
+    def row_copy(to, which):
         return pltpu.make_async_remote_copy(
             src_ref=all_row.at[me],
             dst_ref=all_row.at[me],
-            send_sem=send_taps.at[0, to],
-            recv_sem=recv_row.at[source],
+            send_sem=send_row,
+            recv_sem=recv_row.at[which],
             device_id={"rows": to},
         )
 
-    def col_copy(to, source):
+    def row_relay(to):
+        return pltpu.make_async_remote_copy(
+            src_ref=all_row.at[mirror],
+            dst_ref=all_row.at[mirror],
+            send_sem=send_row,
+            recv_sem=recv_row.at[2],
+            device_id={"rows": to},
+        )
+
+    def rows_moved(amount, which):
+        held = all_row.at[pl.ds(0, amount)]
+        return pltpu.make_async_remote_copy(
+            src_ref=held,
+            dst_ref=held,
+            send_sem=send_row,
+            recv_sem=recv_row.at[which],
+            device_id={"rows": peer(1)},
+        )
+
+    def col_copy(to):
         return pltpu.make_async_remote_copy(
             src_ref=all_column.at[me],
             dst_ref=all_column.at[me],
-            send_sem=send_taps.at[1, to],
-            recv_sem=recv_col.at[source],
+            send_sem=send_col,
+            recv_sem=recv_col,
             device_id={"rows": to},
+        )
+
+    def cols_moved():
+        held = all_column.at[pl.ds(0, count - 1)]
+        return pltpu.make_async_remote_copy(
+            src_ref=held,
+            dst_ref=held,
+            send_sem=send_col,
+            recv_sem=recv_col,
+            device_id={"rows": peer(1)},
         )
 
     def halo_copy(which):
@@ -373,22 +433,57 @@
         over_level(lambda to: px_start(piece, to))
 
     with jax.named_scope("barrier"):
-        pl.semaphore_wait(barrier, count - 1)
+        pl.semaphore_wait(barrier, plane * 4 + 3)
+
+    @pl.loop(0, plane * 4)
+    def _(to):
+        pl.semaphore_signal(hello.at[plane], inc=1, device_id={"rows": to})
+
     with jax.named_scope("loadpx"):
         load_col.wait()
-        load_px.wait()
-
-    over_all(lambda to: col_copy(to, me).start())
-    cross_px(0)
-    beside_px(0)
-    level_px(0)
+        loaded_px(piece_cols, 0)
+
+    def met(other):
+        @pl.when(plane < other)
+        def _():
+            pl.semaphore_wait(hello.at[other], 4)
+
+    def first_out(to):
+        col_copy(to).start()
+        px_start(0, to)
+
+    def first_cross(start, stop):
+        @pl.loop(start, stop)
+        def _(step):
+            first_out(cross(step))
+
+    with jax.named_scope("firstout"):
+
+        @pl.when(low_half)
+        def _():
+            met(1)
+            over_beside(first_out)
+            met(2)
+            first_cross(4, 8)
+            met(3)
+            first_cross(0, 4)
+
+        @pl.when(jnp.logical_not(low_half))
+        def _():
+            first_cross(0, 8)
+            met(3)
+            over_beside(first_out)
+
+        over_level(first_out)
+        load_row.wait()
+        row_copy(mirror, 0).start()
+        loaded_px(cols_dev - piece_cols, 6)
 
     top_row[...] = padded[8:9, :]
     bottom_row[...] = padded[7 + rows_dev : 8 + rows_dev, :]
     halo_copy(0).start()
     halo_copy(1).start()
-    load_row.wait()
-    over_all(lambda to: row_copy(to, me).start())
+    over_half(lambda to: row_copy(to, 1).start())
 
     @pl.when(outer)
     def _():
@@ -410,10 +505,7 @@
     load_stencil.wait()
 
     with jax.named_scope("waitcol"):
-
-        @pl.loop(1, count)
-        def _(step):
-            col_copy(peer(step), peer(step)).wait_recv()
+        cols_moved().wait_recv()
 
     per_block = 128 // rows_dev
     taps = jnp.concatenate([all_column[rank] for rank in range(count)], axis=0)
@@ -487,10 +579,8 @@
         return mm3(loaded(inverse_table), split_bf16(cells))
 
     def filter_spectrum():
-        @pl.loop(1, count)
-        def _(step):
-            row_copy(peer(step), peer(step)).wait_recv()
-
+        rows_moved(count // 2 - 1, 1).wait_recv()
+        rows_moved(count // 2 - 1, 2).wait_recv()
         row_filter = jnp.concatenate([all_row[rank] for rank in range(count)], axis=0)
         nothing = jnp.zeros_like(row_filter)
         filter_spec = spectrum(
@@ -511,7 +601,7 @@
         padded[7:8, :] = halo_above[...]
         padded[8 + rows_dev : 9 + rows_dev, :] = halo_below[...]
         width = side * side
-        for group in range(groups):
+        for group in range(rows_dev // 8):
             base = group * 8
             above = padded[7 + base : 15 + base, :]
             here = padded[8 + base : 16 + base, :]
@@ -527,12 +617,13 @@
     def back_start(group, to, pieces_from, pieces_to):
         width = (pieces_to - pieces_from) * piece_cols
         at = pieces_from * piece_cols
+        row, size = bands[group]
         pltpu.make_async_remote_copy(
             src_ref=ready.at[
-                pl.ds(pl.multiple_of(to * rows_dev + group * 8, 8), 8), pl.ds(at, width)
+                pl.ds(pl.multiple_of(to * rows_dev + row, size), size), pl.ds(at, width)
             ],
             dst_ref=back.at[
-                pl.ds(group * 8, 8), pl.ds(pl.multiple_of(me * cols_dev + at, 128), width)
+                pl.ds(row, size), pl.ds(pl.multiple_of(me * cols_dev + at, 128), width)
             ],
             send_sem=send_back,
             recv_sem=recv_back.at[group],
@@ -540,7 +631,8 @@
         ).start()
 
     def back_all(group):
-        held = back.at[pl.ds(group * 8, 8), pl.ds(0, (count - 1) * cols_dev)]
+        row, size = bands[group]
+        held = back.at[pl.ds(row, size), pl.ds(0, (count - 1) * cols_dev)]
         return pltpu.make_async_remote_copy(
             src_ref=held,
             dst_ref=held,
@@ -549,14 +641,24 @@
             device_id={"rows": peer(1)},
         )
 
+    def all_sent(sem):
+        held = recv.at[:, pl.ds(0, column_length - rows_dev), :]
+        pltpu.make_async_remote_copy(
+            src_ref=held,
+            dst_ref=held,
+            send_sem=sem,
+            recv_sem=recv_px.at[0],
+            device_id={"rows": peer(1)},
+        ).wait_send()
+
     def rest(group):
         def start(to):
             back_start(group, to, last if group == 0 else 0, pieces)
 
         return start
 
-    def early(piece):
-        over_all(lambda to: back_start(0, to, piece, piece + 1))
+    def early():
+        over_all(lambda to: back_start(0, to, 0, last))
 
     for piece in range(pieces):
         with jax.named_scope(f"waitpx#p={piece}"):
@@ -567,8 +669,7 @@
             cross_px(piece + 1)
             beside_px(piece + 2)
             if piece == last:
-                for sent in range(last):
-                    early(sent)
+                early()
 
         with jax.named_scope(f"mm#p={piece}"):
             high, low = split_bf16(recv[piece])
@@ -578,16 +679,20 @@
             ready[:, at] = mm3(
                 (circ_high[...], circ_low[...]), (part_high[...], part_low[...])
             )
-        if piece != last:
+        if piece == last - 1:
 
             @pl.when(inner)
-            def _(piece=piece):
-                early(piece)
+            def _():
+                early()
 
         if piece == 0:
             with jax.named_scope("stencil"):
                 add_stencil()
         if piece == 1:
+            with jax.named_scope("relay"):
+                rows_moved(1, 0).wait_recv()
+                over_half(lambda to: row_relay(to).start())
+        if piece == 2:
             with jax.named_scope("filtspec"):
                 filter_spectrum()
 
@@ -609,27 +714,36 @@
 
     flat_cells = cells_by_row.reshape(rows_dev * side, side)
     for group in range(groups):
+        if group == 1:
+            all_sent(send_px)
+            rows_moved(count - 1, 0).wait_send()
+            cols_moved().wait_send()
+            halo_copy(0).wait_send()
+            halo_copy(1).wait_send()
         with jax.named_scope(f"waitback#g={group}"):
             back_all(group).wait_recv()
 
         @pl.when(outer)
         def _(group=group):
-            if group + 1 < groups:
+            if group + 1 < groups - 2:
                 over_cross(rest(group + 1))
-            if group + 2 < groups:
                 over_beside(rest(group + 2))
-
+            if group == groups - 3:
+                over_cross(rest(group + 1))
+                over_cross(rest(group + 2))
+                over_beside(rest(group + 2))
+
+        row, size = bands[group]
         with jax.named_scope(f"fft#g={group}"):
             for a in range(side):
-                flat_cells[pl.ds(group * 8 * side + a, 8, stride=side), :] = back[
-                    group * 8 : group * 8 + 8, a * side : (a + 1) * side
+                flat_cells[pl.ds(row * side + a, size, stride=side), :] = back[
+                    row : row + size, a * side : (a + 1) * side
                 ]
-            for half in range(2):
-                row = group * 8 + half * 4
+            for at in range(row, row + size, 4):
                 cells = jnp.concatenate(
                     [
-                        jnp.concatenate([cells_by_row[row], cells_by_row[row + 2]], axis=1),
-                        jnp.concatenate([cells_by_row[row + 1], cells_by_row[row + 3]], axis=1),
+                        jnp.concatenate([cells_by_row[at], cells_by_row[at + 2]], axis=1),
+                        jnp.concatenate([cells_by_row[at + 1], cells_by_row[at + 3]], axis=1),
                     ],
                     axis=0,
                 )
@@ -638,28 +752,20 @@
                 filt_r = jnp.concatenate([filter_real[...]] * 2, axis=0)
                 filt_i = jnp.concatenate([filter_imag[...]] * 2, axis=0)
                 done = inverse_of(real * filt_r - imag * filt_i, real * filt_i + imag * filt_r)
-                cells_by_row[row] = done[:side, :side]
-                cells_by_row[row + 1] = done[side:, :side]
-                cells_by_row[row + 2] = done[:side, side:]
-                cells_by_row[row + 3] = done[side:, side:]
-            for a in range(side):
-                cut = slice(a * side, (a + 1) * side)
-                out[group * 8 : group * 8 + 8, cut] += flat_cells[
-                    pl.ds(group * 8 * side + a, 8, stride=side), :
-                ]
+                cells_by_row[at] = done[:side, :side]
+                cells_by_row[at + 1] = done[side:, :side]
+                cells_by_row[at + 2] = done[:side, side:]
+                cells_by_row[at + 3] = done[side:, side:]
+            if (row + size) % 8 == 0:
+                base = row + size - 8
+                for a in range(side):
+                    cut = slice(a * side, (a + 1) * side)
+                    out[base : base + 8, cut] += flat_cells[
+                        pl.ds(base * side + a, 8, stride=side), :
+                    ]
 
     with jax.named_scope("drain"):
-        halo_copy(0).wait_send()
-        halo_copy(1).wait_send()
-        for piece in range(pieces):
-            px_all(piece).wait_send()
-        for group in range(groups):
-            back_all(group).wait_send()
-
-        @pl.loop(1, count)
-        def _(step):
-            row_copy(peer(step), peer(step)).wait_send()
-            col_copy(peer(step), peer(step)).wait_send()
+        all_sent(send_back)
 
 
 def fits(pixels, row_taps, column_taps):
@@ -685,7 +791,7 @@
     column_length = rows_dev * count
     cols_dev = row_length // count
     a_dev = cols_dev // 128
-    groups = rows_dev // 8
+    groups = len(bands_of(rows_dev))
     pieces = 4
     piece_cols = cols_dev // pieces
     made = host_tables(side)
@@ -723,14 +829,16 @@
             pltpu.SMEM((3, 3), f32),
             dma,
             dma((pieces,)),
-            dma((2, count)),
-            dma((count,)),
-            dma((count,)),
+            dma,
+            dma,
+            dma((3,)),
+            dma,
             dma((2,)),
             dma((2,)),
             dma,
             dma((groups,)),
-            dma((6,)),
+            dma((7,)),
+            pltpu.SemaphoreType.REGULAR((4,)),
         ],
         compiler_params=pltpu.CompilerParams(
             collective_id=0, has_side_effects=True, vmem_limit_bytes=32 * 1024 * 1024

time: 104 us -> 99.9 us (0.961)
  Pallas kernels: 102 us -> 98.4 us
    pallas_call x1, Pallas kernels: 102 us -> 98.4 us  [fused(): pl.pallas_call(functools.partial(kernel, (count, rows_dev, side, pieces))...]
where the time goes in v2:
time: 99.9 us; the launch traced here: 99.8 us
  Pallas kernels  98.4 us (98%)
  local copies, waits for them, and re-layouts  1.32 us (1%)
    pallas_call x1, Pallas kernels, fused(): pl.pallas_call(functools.partial(kernel, (count, rows_dev, side, pieces))...  98.4 us

profile of v2, /device:TPU:0, one launch (start us, length us, event | category | flops | bytes accessed | tf_op | source)
XLA Modules:
  0.0 99.8 jit_solution(9267976906228296694)
XLA Ops:
  0.0 98.4 %shard_map.64 = f32[32,16384]{1,0:T(8,128)S(1)} custom-call(f32[32,16384]{1,0:T(8,128)} %pixels.1, f32[8,128]{1,0:T(8,128)} %bitcast.2, f32[1,32]{1,0:T(1,128)} %bitcast.3, f32[3,3]{1,0:T(4,128)} %stencil_in.1, bf16[4,256,256]{2,1,0:T(8,128)(2,1)} %constant.4.clone.tables_in, f32[2,128,128]{2,1,0:T(8,128)} %constant.5.clone.twists_in), custom_call_target="tpu_custom_call" | custom-call | tf_op jit(solution)/shard_map/pallas_call | solution.py:804
  98.4 1.3 %copy.8 = f32[32,16384]{1,0:T(8,128)} copy(f32[32,16384]{1,0:T(8,128)S(1)} %shard_map.64) | data formatting | bytes 4194304

commit v3 on v2

--- a/solution.py
+++ b/solution.py
@@ -196,8 +196,12 @@
 
 
 def bands_of(rows_dev):
-    whole = [(at, 8) for at in range(0, rows_dev - 8, 8)]
-    return whole + [(rows_dev - 8, 4), (rows_dev - 4, 4)]
+    return [(at, 8) for at in range(0, rows_dev, 8)]
+
+
+def cuts_of(cols_dev):
+    step = cols_dev // 4
+    return [(at, step) for at in range(0, cols_dev, step)]
 
 
 def kernel(
@@ -242,13 +246,14 @@
     local_sem,
     hello,
 ):
-    count, rows_dev, side, pieces = dims
+    count, rows_dev, side = dims
     bands = bands_of(rows_dev)
     groups = len(bands)
     cols_dev = side * side // count
     a_dev = cols_dev // 128
     column_length = count * rows_dev
-    piece_cols = cols_dev // pieces
+    cuts = cuts_of(cols_dev)
+    pieces = len(cuts)
     last = pieces - 1
     own = slice(8, 8 + rows_dev)
     me = lax.axis_index("rows")
@@ -260,8 +265,8 @@
     first = jnp.where(low_half, core, 1 - core)
 
     def cross(step):
-        turn = lax.rem(step // 2 + first, 2)
-        depth = step // 4
+        turn = lax.rem(step // 4 + first, 2)
+        depth = lax.rem(step // 2, 2)
         plane_to = jnp.where(low_half, 3 - depth, depth)
         return plane_to * 4 + lax.rem(x + turn, 2) * 2 + lax.rem(core + step, 2)
 
@@ -280,6 +285,15 @@
         def _(step):
             start(cross(step))
 
+    def over_cross_last(start):
+        @pl.loop(0, 8)
+        def _(step):
+            major, minor = step // 4, lax.rem(step // 2, 2)
+            depth = jnp.where(low_half, minor, major)
+            side_to = jnp.where(low_half, major, minor)
+            plane_to = jnp.where(low_half, 2, 0) + depth
+            start(plane_to * 4 + side_to * 2 + lax.rem(core + step, 2))
+
     def over_beside(start):
         @pl.loop(0, 4)
         def _(step):
@@ -302,9 +316,11 @@
     mirror = lax.rem(me + count // 2, count)
     barrier = pltpu.get_barrier_semaphore()
 
-    over_level(lambda to: pl.semaphore_signal(barrier, inc=1, device_id={"rows": to}))
-
-    @pl.loop((plane + 1) * 4, count)
+    chip = me // 2
+    partner = chip * 2 + 1 - core
+    pl.semaphore_signal(barrier, inc=1, device_id={"rows": partner})
+
+    @pl.loop((chip + 1) * 2, count)
     def _(to):
         pl.semaphore_signal(barrier, inc=1, device_id={"rows": to})
 
@@ -325,20 +341,21 @@
 
     @pl.loop(0, count)
     def _(rank):
-        load_part(rank, 0, piece_cols, 0).start()
+        load_part(rank, 0, cuts[1][0], 0).start()
 
     load_row.start()
 
     @pl.loop(0, count)
     def _(rank):
-        load_part(rank, piece_cols, cols_dev - piece_cols, 6).start()
+        load_part(rank, cuts[1][0], cols_dev - cuts[1][0], 6).start()
 
     load_tables.start()
     load_twists.start()
     load_stencil.start()
 
     def columns_of(rank, piece):
-        return pl.ds(pl.multiple_of(rank * cols_dev + piece * piece_cols, 128), piece_cols)
+        at, width = cuts[piece]
+        return pl.ds(pl.multiple_of(rank * cols_dev + at, 128), width)
 
     def all_columns_of(rank):
         return pl.ds(pl.multiple_of(rank * cols_dev, 128), cols_dev)
@@ -349,14 +366,14 @@
     def px_start(piece, to):
         pltpu.make_async_remote_copy(
             src_ref=padded.at[own, columns_of(to, piece)],
-            dst_ref=recv.at[piece, rows_of(me), :],
+            dst_ref=recv.at[rows_of(me), pl.ds(*cuts[piece])],
             send_sem=send_px,
             recv_sem=recv_px.at[piece],
             device_id={"rows": to},
         ).start()
 
     def px_all(piece):
-        held = recv.at[piece, pl.ds(0, column_length - rows_dev), :]
+        held = recv.at[pl.ds(0, column_length - rows_dev), pl.ds(*cuts[piece])]
         return pltpu.make_async_remote_copy(
             src_ref=held,
             dst_ref=held,
@@ -433,51 +450,57 @@
         over_level(lambda to: px_start(piece, to))
 
     with jax.named_scope("barrier"):
-        pl.semaphore_wait(barrier, plane * 4 + 3)
-
-    @pl.loop(0, plane * 4)
+        pl.semaphore_wait(barrier, chip * 2 + 1)
+
+    @pl.loop(0, chip * 2)
     def _(to):
-        pl.semaphore_signal(hello.at[plane], inc=1, device_id={"rows": to})
+        pl.semaphore_signal(hello.at[chip], inc=1, device_id={"rows": to})
 
     with jax.named_scope("loadpx"):
         load_col.wait()
-        loaded_px(piece_cols, 0)
-
-    def met(other):
-        @pl.when(plane < other)
-        def _():
-            pl.semaphore_wait(hello.at[other], 4)
-
-    def first_out(to):
-        col_copy(to).start()
-        px_start(0, to)
-
-    def first_cross(start, stop):
-        @pl.loop(start, stop)
-        def _(step):
-            first_out(cross(step))
+        load_row.wait()
+        loaded_px(cuts[1][0], 0)
 
     with jax.named_scope("firstout"):
+
+        def met(other):
+            @pl.when(chip < other)
+            def _():
+                pl.semaphore_wait(hello.at[other], 2)
+
+        def first_out(to):
+            @pl.when(to == mirror)
+            def _():
+                row_copy(mirror, 0).start()
+
+            col_copy(to).start()
+            px_start(0, to)
+
+        def first_pairs(pairs, target):
+            @pl.loop(0, pairs)
+            def _(pair):
+                to = target(pair * 2)
+                met(to // 2)
+                first_out(to)
+                first_out(target(pair * 2 + 1))
+
+        def risen(step):
+            turn = lax.rem(step // 2 + first, 2)
+            return (2 + step // 4) * 4 + lax.rem(x + turn, 2) * 2 + lax.rem(core + step, 2)
 
         @pl.when(low_half)
         def _():
-            met(1)
-            over_beside(first_out)
-            met(2)
-            first_cross(4, 8)
-            met(3)
-            first_cross(0, 4)
+            first_pairs(2, beside)
+            first_pairs(4, risen)
 
         @pl.when(jnp.logical_not(low_half))
         def _():
-            first_cross(0, 8)
-            met(3)
-            over_beside(first_out)
-
+            first_pairs(4, cross)
+            first_pairs(2, beside)
+
+        met(chip + 1 - 2 * x)
         over_level(first_out)
-        load_row.wait()
-        row_copy(mirror, 0).start()
-        loaded_px(cols_dev - piece_cols, 6)
+        loaded_px(cols_dev - cuts[1][0], 6)
 
     top_row[...] = padded[8:9, :]
     bottom_row[...] = padded[7 + rows_dev : 8 + rows_dev, :]
@@ -498,8 +521,7 @@
     for piece in range(1, pieces):
         level_px(piece)
 
-    for piece in range(pieces):
-        recv[piece, rows_of(me), :] = padded[own, columns_of(me, piece)]
+    recv[rows_of(me), :] = padded[own, all_columns_of(me)]
     load_tables.wait()
     load_twists.wait()
     load_stencil.wait()
@@ -553,15 +575,17 @@
             axis=0,
         )
 
-    def spectrum(cells):
+    def first_turn(cells):
         first = mm3(loaded(forward_table), split_bf16(cells))
         real, imag = first[:side], first[side:]
         turn_r = jnp.concatenate([twists[0]] * 2, axis=1)
         turn_i = jnp.concatenate([twists[1]] * 2, axis=1)
-        turned_cells = swap(real * turn_r - imag * turn_i, real * turn_i + imag * turn_r)
-        return mm3(split_bf16(turned_cells), loaded(inverse_table))
-
-    def inverse_of(real, imag):
+        return swap(real * turn_r - imag * turn_i, real * turn_i + imag * turn_r)
+
+    def spectrum(cells):
+        return mm3(split_bf16(first_turn(cells)), loaded(inverse_table))
+
+    def back_turn(real, imag):
         cells = jnp.concatenate([real, imag], axis=1)
         first = mm3(split_bf16(cells), loaded(forward_table))
         real, imag = first[:, :side], first[:, side:]
@@ -569,14 +593,13 @@
         turn_i = jnp.concatenate([twists[1]] * 2, axis=0)
         back_real = real * turn_r + imag * turn_i
         back_imag = imag * turn_r - real * turn_i
-        cells = jnp.concatenate(
+        return jnp.concatenate(
             [
                 jnp.concatenate([back_real[:side], back_real[side:]], axis=1),
                 jnp.concatenate([back_imag[:side], back_imag[side:]], axis=1),
             ],
             axis=0,
         )
-        return mm3(loaded(inverse_table), split_bf16(cells))
 
     def filter_spectrum():
         rows_moved(count // 2 - 1, 1).wait_recv()
@@ -614,9 +637,7 @@
                 sums[1] + pltpu.roll(sums[0], 1, 1) + pltpu.roll(sums[2], width - 1, 1)
             )
 
-    def back_start(group, to, pieces_from, pieces_to):
-        width = (pieces_to - pieces_from) * piece_cols
-        at = pieces_from * piece_cols
+    def back_start(group, to, at, width):
         row, size = bands[group]
         pltpu.make_async_remote_copy(
             src_ref=ready.at[
@@ -642,7 +663,7 @@
         )
 
     def all_sent(sem):
-        held = recv.at[:, pl.ds(0, column_length - rows_dev), :]
+        held = recv.at[pl.ds(0, column_length - rows_dev), :]
         pltpu.make_async_remote_copy(
             src_ref=held,
             dst_ref=held,
@@ -653,12 +674,13 @@
 
     def rest(group):
         def start(to):
-            back_start(group, to, last if group == 0 else 0, pieces)
+            at = cuts[last][0] if group == 0 else 0
+            back_start(group, to, at, cols_dev - at)
 
         return start
 
     def early():
-        over_all(lambda to: back_start(0, to, 0, last))
+        over_all(lambda to: back_start(0, to, 0, cuts[last][0]))
 
     for piece in range(pieces):
         with jax.named_scope(f"waitpx#p={piece}"):
@@ -672,12 +694,12 @@
                 early()
 
         with jax.named_scope(f"mm#p={piece}"):
-            high, low = split_bf16(recv[piece])
-            part_high[...] = high
-            part_low[...] = low
-            at = slice(piece * piece_cols, (piece + 1) * piece_cols)
-            ready[:, at] = mm3(
-                (circ_high[...], circ_low[...]), (part_high[...], part_low[...])
+            at, width = cuts[piece]
+            high, low = split_bf16(recv[:, at : at + width])
+            part_high[:, :width] = high
+            part_low[:, :width] = low
+            ready[:, at : at + width] = mm3(
+                (circ_high[...], circ_low[...]), (part_high[:, :width], part_low[:, :width])
             )
         if piece == last - 1:
 
@@ -692,9 +714,6 @@
             with jax.named_scope("relay"):
                 rows_moved(1, 0).wait_recv()
                 over_half(lambda to: row_relay(to).start())
-        if piece == 2:
-            with jax.named_scope("filtspec"):
-                filter_spectrum()
 
     @pl.when(outer)
     def _():
@@ -704,13 +723,17 @@
 
     @pl.when(inner)
     def _():
-        for group in range(groups):
+        for group in range(groups - 1):
             over_cross(rest(group))
             over_beside(rest(group))
+        over_cross_last(rest(groups - 1))
+        over_beside(rest(groups - 1))
 
     for group in range(groups):
         over_level(rest(group))
     back[:, all_columns_of(me)] = ready[rows_of(me), :]
+    with jax.named_scope("filtspec"):
+        filter_spectrum()
 
     flat_cells = cells_by_row.reshape(rows_dev * side, side)
     for group in range(groups):
@@ -725,12 +748,11 @@
 
         @pl.when(outer)
         def _(group=group):
-            if group + 1 < groups - 2:
+            if group + 1 < groups - 1:
                 over_cross(rest(group + 1))
-                over_beside(rest(group + 2))
-            if group == groups - 3:
-                over_cross(rest(group + 1))
-                over_cross(rest(group + 2))
+            if group + 1 == groups - 1:
+                over_cross_last(rest(group + 1))
+            if group + 2 < groups:
                 over_beside(rest(group + 2))
 
         row, size = bands[group]
@@ -739,19 +761,31 @@
                 flat_cells[pl.ds(row * side + a, size, stride=side), :] = back[
                     row : row + size, a * side : (a + 1) * side
                 ]
-            for at in range(row, row + size, 4):
-                cells = jnp.concatenate(
+            filt_r = jnp.concatenate([filter_real[...]] * 2, axis=0)
+            filt_i = jnp.concatenate([filter_imag[...]] * 2, axis=0)
+            starts = range(row, row + size, 4)
+            held = [
+                jnp.concatenate(
                     [
                         jnp.concatenate([cells_by_row[at], cells_by_row[at + 2]], axis=1),
                         jnp.concatenate([cells_by_row[at + 1], cells_by_row[at + 3]], axis=1),
                     ],
                     axis=0,
                 )
-                spec = spectrum(cells)
-                real, imag = spec[:, :side], spec[:, side:]
-                filt_r = jnp.concatenate([filter_real[...]] * 2, axis=0)
-                filt_i = jnp.concatenate([filter_imag[...]] * 2, axis=0)
-                done = inverse_of(real * filt_r - imag * filt_i, real * filt_i + imag * filt_r)
+                for at in starts
+            ]
+            held = [first_turn(cells) for cells in held]
+            held = [mm3(split_bf16(cells), loaded(inverse_table)) for cells in held]
+            held = [
+                (
+                    spec[:, :side] * filt_r - spec[:, side:] * filt_i,
+                    spec[:, :side] * filt_i + spec[:, side:] * filt_r,
+                )
+                for spec in held
+            ]
+            held = [back_turn(real, imag) for real, imag in held]
+            held = [mm3(loaded(inverse_table), split_bf16(cells)) for cells in held]
+            for at, done in zip(starts, held):
                 cells_by_row[at] = done[:side, :side]
                 cells_by_row[at + 1] = done[side:, :side]
                 cells_by_row[at + 2] = done[:side, side:]
@@ -792,8 +826,8 @@
     cols_dev = row_length // count
     a_dev = cols_dev // 128
     groups = len(bands_of(rows_dev))
-    pieces = 4
-    piece_cols = cols_dev // pieces
+    cuts = cuts_of(cols_dev)
+    pieces = len(cuts)
     made = host_tables(side)
     tables = jnp.asarray(np.stack(made[:4]))
     twists = jnp.asarray(np.stack(made[4:]))
@@ -802,7 +836,7 @@
     f32, bf16 = jnp.float32, jnp.bfloat16
     dma = pltpu.SemaphoreType.DMA
     return pl.pallas_call(
-        functools.partial(kernel, (count, rows_dev, side, pieces)),
+        functools.partial(kernel, (count, rows_dev, side)),
         out_shape=jax.ShapeDtypeStruct(pixels.shape, f32),
         in_specs=[hbm] * 6,
         out_specs=vmem,
@@ -812,9 +846,9 @@
             pltpu.VMEM(twists.shape, f32),
             pltpu.VMEM((1, row_length), f32),
             pltpu.VMEM((1, row_length), f32),
-            pltpu.VMEM((pieces, column_length, piece_cols), f32),
-            pltpu.VMEM((column_length, piece_cols), bf16),
-            pltpu.VMEM((column_length, piece_cols), bf16),
+            pltpu.VMEM((column_length, cols_dev), f32),
+            pltpu.VMEM((column_length, cuts[0][1]), bf16),
+            pltpu.VMEM((column_length, cuts[0][1]), bf16),
             pltpu.VMEM((column_length, cols_dev), f32),
             pltpu.VMEM((rows_dev, row_length), f32),
             pltpu.VMEM((rows_dev, side, side), f32),
@@ -838,7 +872,7 @@
             dma,
             dma((groups,)),
             dma((7,)),
-            pltpu.SemaphoreType.REGULAR((4,)),
+            pltpu.SemaphoreType.REGULAR((count // 2,)),
         ],
         compiler_params=pltpu.CompilerParams(
             collective_id=0, has_side_effects=True, vmem_limit_bytes=32 * 1024 * 1024

time: 99.9 us -> 99.1 us (level); the launches traced: 99.8 us -> 97.4 us
  Pallas kernels: 98.4 us -> 96.1 us
    pallas_call x1, Pallas kernels: 98.4 us -> 96.1 us  [fused(): pl.pallas_call(functools.partial(kernel, (count, rows_dev, side)), out_sh...]
where the time goes in v3:
time: 99.1 us; the launch traced here: 97.4 us
  Pallas kernels  96.1 us (97%)
  local copies, waits for them, and re-layouts  1.32 us (1%)
    pallas_call x1, Pallas kernels, fused(): pl.pallas_call(functools.partial(kernel, (count, rows_dev, side)), out_sh...  96.1 us

profile of v3, /device:TPU:0, one launch (start us, length us, event | category | flops | bytes accessed | tf_op | source)
XLA Modules:
  0.0 97.4 jit_solution(1976071593400714326)
XLA Ops:
  0.0 96.1 %shard_map.64 = f32[32,16384]{1,0:T(8,128)S(1)} custom-call(f32[32,16384]{1,0:T(8,128)} %pixels.1, f32[8,128]{1,0:T(8,128)} %bitcast.2, f32[1,32]{1,0:T(1,128)} %bitcast.3, f32[3,3]{1,0:T(4,128)} %stencil_in.1, bf16[4,256,256]{2,1,0:T(8,128)(2,1)} %constant.4.clone.tables_in, f32[2,128,128]{2,1,0:T(8,128)} %constant.5.clone.twists_in), custom_call_target="tpu_custom_call" | custom-call | tf_op jit(solution)/shard_map/pallas_call | solution.py:838
  96.1 1.3 %copy.8 = f32[32,16384]{1,0:T(8,128)} copy(f32[32,16384]{1,0:T(8,128)S(1)} %shard_map.64) | data formatting | bytes 4194304

commit v4 on v3

--- a/solution.py
+++ b/solution.py
@@ -345,14 +345,6 @@
 
     load_row.start()
 
-    @pl.loop(0, count)
-    def _(rank):
-        load_part(rank, cuts[1][0], cols_dev - cuts[1][0], 6).start()
-
-    load_tables.start()
-    load_twists.start()
-    load_stencil.start()
-
     def columns_of(rank, piece):
         at, width = cuts[piece]
         return pl.ds(pl.multiple_of(rank * cols_dev + at, 128), width)
@@ -455,6 +447,14 @@
     @pl.loop(0, chip * 2)
     def _(to):
         pl.semaphore_signal(hello.at[chip], inc=1, device_id={"rows": to})
+
+    @pl.loop(0, count)
+    def _(rank):
+        load_part(rank, cuts[1][0], cols_dev - cuts[1][0], 6).start()
+
+    load_tables.start()
+    load_twists.start()
+    load_stencil.start()
 
     with jax.named_scope("loadpx"):
         load_col.wait()
@@ -735,7 +735,11 @@
     with jax.named_scope("filtspec"):
         filter_spectrum()
 
-    flat_cells = cells_by_row.reshape(rows_dev * side, side)
+    pitch = side + 8
+
+    def cells_of(row):
+        return slice(row * pitch, row * pitch + side)
+
     for group in range(groups):
         if group == 1:
             all_sent(send_px)
@@ -758,7 +762,7 @@
         row, size = bands[group]
         with jax.named_scope(f"fft#g={group}"):
             for a in range(side):
-                flat_cells[pl.ds(row * side + a, size, stride=side), :] = back[
+                cells_by_row[pl.ds(row * pitch + a, size, stride=pitch), :] = back[
                     row : row + size, a * side : (a + 1) * side
                 ]
             filt_r = jnp.concatenate([filter_real[...]] * 2, axis=0)
@@ -767,8 +771,12 @@
             held = [
                 jnp.concatenate(
                     [
-                        jnp.concatenate([cells_by_row[at], cells_by_row[at + 2]], axis=1),
-                        jnp.concatenate([cells_by_row[at + 1], cells_by_row[at + 3]], axis=1),
+                        jnp.concatenate(
+                            [cells_by_row[cells_of(at)], cells_by_row[cells_of(at + 2)]], axis=1
+                        ),
+                        jnp.concatenate(
+                            [cells_by_row[cells_of(at + 1)], cells_by_row[cells_of(at + 3)]], axis=1
+                        ),
                     ],
                     axis=0,
                 )
@@ -786,16 +794,16 @@
             held = [back_turn(real, imag) for real, imag in held]
             held = [mm3(loaded(inverse_table), split_bf16(cells)) for cells in held]
             for at, done in zip(starts, held):
-                cells_by_row[at] = done[:side, :side]
-                cells_by_row[at + 1] = done[side:, :side]
-                cells_by_row[at + 2] = done[:side, side:]
-                cells_by_row[at + 3] = done[side:, side:]
+                cells_by_row[cells_of(at)] = done[:side, :side]
+                cells_by_row[cells_of(at + 1)] = done[side:, :side]
+                cells_by_row[cells_of(at + 2)] = done[:side, side:]
+                cells_by_row[cells_of(at + 3)] = done[side:, side:]
             if (row + size) % 8 == 0:
                 base = row + size - 8
                 for a in range(side):
                     cut = slice(a * side, (a + 1) * side)
-                    out[base : base + 8, cut] += flat_cells[
-                        pl.ds(base * side + a, 8, stride=side), :
+                    out[base : base + 8, cut] += cells_by_row[
+                        pl.ds(base * pitch + a, 8, stride=pitch), :
                     ]
 
     with jax.named_scope("drain"):
@@ -851,7 +859,7 @@
             pltpu.VMEM((column_length, cuts[0][1]), bf16),
             pltpu.VMEM((column_length, cols_dev), f32),
             pltpu.VMEM((rows_dev, row_length), f32),
-            pltpu.VMEM((rows_dev, side, side), f32),
+            pltpu.VMEM((rows_dev * (side + 8), side), f32),
             pltpu.VMEM((1, row_length), f32),
             pltpu.VMEM((1, row_length), f32),
             pltpu.VMEM((count, a_dev, 128), f32),

time: 99.1 us -> 98.8 us (level)
  no operation moved by 1% of the time
where the time goes in v4:
time: 98.8 us; the launch traced here: 97.1 us
  Pallas kernels  95.7 us (97%)
  local copies, waits for them, and re-layouts  1.32 us (1%)
    pallas_call x1, Pallas kernels, fused(): pl.pallas_call(functools.partial(kernel, (count, rows_dev, side)), out_sh...  95.7 us

profile of v4, /device:TPU:0, one launch (start us, length us, event | category | flops | bytes accessed | tf_op | source)
XLA Modules:
  0.0 97.1 jit_solution(9282756302144674478)
XLA Ops:
  0.0 95.7 %shard_map.64 = f32[32,16384]{1,0:T(8,128)S(1)} custom-call(f32[32,16384]{1,0:T(8,128)} %pixels.1, f32[8,128]{1,0:T(8,128)} %bitcast.2, f32[1,32]{1,0:T(1,128)} %bitcast.3, f32[3,3]{1,0:T(4,128)} %stencil_in.1, bf16[4,256,256]{2,1,0:T(8,128)(2,1)} %constant.4.clone.tables_in, f32[2,128,128]{2,1,0:T(8,128)} %constant.5.clone.twists_in), custom_call_target="tpu_custom_call" | custom-call | tf_op jit(solution)/shard_map/pallas_call | solution.py:846
  95.8 1.3 %copy.8 = f32[32,16384]{1,0:T(8,128)} copy(f32[32,16384]{1,0:T(8,128)S(1)} %shard_map.64) | data formatting | bytes 4194304

commit v5 on v4

--- a/solution.py
+++ b/solution.py
@@ -688,7 +688,10 @@
 
         @pl.when(outer)
         def _(piece=piece):
-            cross_px(piece + 1)
+            if piece != last - 1:
+                cross_px(piece + 1)
+            if piece == last - 2:
+                cross_px(last)
             beside_px(piece + 2)
             if piece == last:
                 early()

time: 98.8 us -> 98.7 us (level)
  no operation moved by 1% of the time
where the time goes in v5:
time: 98.7 us; the launch traced here: 97.2 us
  Pallas kernels  95.8 us (97%)
  local copies, waits for them, and re-layouts  1.32 us (1%)
    pallas_call x1, Pallas kernels, fused(): pl.pallas_call(functools.partial(kernel, (count, rows_dev, side)), out_sh...  95.8 us

profile of v5, /device:TPU:0, one launch (start us, length us, event | category | flops | bytes accessed | tf_op | source)
XLA Modules:
  0.0 97.2 jit_solution(770631790788777143)
XLA Ops:
  0.0 95.8 %shard_map.64 = f32[32,16384]{1,0:T(8,128)S(1)} custom-call(f32[32,16384]{1,0:T(8,128)} %pixels.1, f32[8,128]{1,0:T(8,128)} %bitcast.2, f32[1,32]{1,0:T(1,128)} %bitcast.3, f32[3,3]{1,0:T(4,128)} %stencil_in.1, bf16[4,256,256]{2,1,0:T(8,128)(2,1)} %constant.4.clone.tables_in, f32[2,128,128]{2,1,0:T(8,128)} %constant.5.clone.twists_in), custom_call_target="tpu_custom_call" | custom-call | tf_op jit(solution)/shard_map/pallas_call | solution.py:849
  95.9 1.3 %copy.8 = f32[32,16384]{1,0:T(8,128)} copy(f32[32,16384]{1,0:T(8,128)S(1)} %shard_map.64) | data formatting | bytes 4194304
